TPU v7x, 256 devices: a 2x2x32 block of a 4x8x32 slice. The times are simulated.
256 devices in a mesh: parts: 4 (over y, x), dp: 64 (over z, core).
Axes of the slice: x: 2, y: 2, z: 32, core: 2. Of those that a mesh axis runs over, the one named last changes fastest.
The devices are a block of a 4x8x32 slice.
Arguments:
- activations: bfloat16 [65536, 14336], P(('parts', 'dp')), parts along dimension 0, may hold values from -6 to 6
- out_grads: bfloat16 [65536, 4096], P(('parts', 'dp')), parts along dimension 0, may hold values from -6 to 6
- lengths: int32 [256, 4], P(('parts', 'dp')), parts along dimension 0, may hold values from 1 to 128, 256 in all within a row
- proj_in: bfloat16 [14336, 64], replicated, may hold values from -0.046875 to 0.046875
- proj_out: bfloat16 [4096, 64], replicated, may hold values from -0.09375 to 0.09375
- queries: bfloat16 [8192, 4096], P(('parts', 'dp')), parts along dimension 0, may hold values from -0.01171875 to 0.01171875
Outputs:
- scores: bfloat16 [1024, 2048], P(('parts', 'dp')), parts along dimension 0
There are 4 independent parts, one for each index of `parts`. A program takes and returns all parts, laid end to end along the dimension named above; an argument that names none is the same for every part. Nothing has to cross between parts.
Inputs may be any that keep to these rules, and one draw needn't show every extreme that they name: Each row of lengths sums to 256, and one entry of each row equals 128.
All inputs are finite; a program needn't handle non-finite values.
Results may differ from a plain program's by a relative error of at most 0.0065.
Values may be sent and summed in bfloat16 or wider, within the bound.
A program may use at most 128 MiB of HBM per device.

v0:
```python
import jax
import jax.numpy as jnp
from jax import lax
from jax.sharding import PartitionSpec as P


def local(activations, out_grads, lengths, proj_in, proj_out, queries):
    tok_count = activations.shape[0]
    rank_size = proj_in.shape[1]
    proj_acts = jnp.dot(activations, proj_in, preferred_element_type=jnp.float32).astype(
        jnp.bfloat16
    )
    proj_grads = jnp.dot(out_grads, proj_out, preferred_element_type=jnp.float32).astype(
        jnp.bfloat16
    )
    counts = lengths[0]
    tok_ends = jnp.cumsum(counts)
    tok_starts = tok_ends - counts
    position = jnp.arange(tok_count, dtype=jnp.int32)
    member = (
        (position[None, :] >= tok_starts[:, None]) & (position[None, :] < tok_ends[:, None])
    ).astype(jnp.bfloat16)
    masked_grads = member[:, :, None] * proj_grads[None, :, :]
    summed = jnp.einsum("eti,tj->eij", masked_grads, proj_acts, preferred_element_type=jnp.float32)
    example_grads = summed.reshape(counts.shape[0], rank_size * rank_size).astype(jnp.bfloat16)
    contract = (((1,), (1,)), ((), ()))
    scores = lax.dot_general(
        example_grads,
        lax.all_gather(queries, "dp", axis=0, tiled=True),
        contract,
        preferred_element_type=jnp.float32,
    )
    return scores.astype(jnp.bfloat16)


def solution(mesh):
    in_specs = (
        P(("parts", "dp"), None),
        P(("parts", "dp"), None),
        P(("parts", "dp"), None),
        P(),
        P(),
        P(("parts", "dp"), None),
    )
    out_specs = P(("parts", "dp"), None)
    return jax.shard_map(local, mesh=mesh, in_specs=in_specs, out_specs=out_specs, check_vma=False)
```

profile of v0, /device:TPU:44, one launch (start us, length us, event | category | flops | bytes accessed | tf_op | source)
XLA Modules:
  0.0 186.6 jit_solution(3009798860218271106)
XLA Ops:
  6.5 0.0 copy-start
  6.6 0.0 all-gather.2.cloned.1.call-start
  6.6 0.7 all-gather.2.cloned.1.call-update
  7.3 0.8 reduce-window.7
  8.1 0.7 bitcast_subtract_fusion
  8.8 0.1 fusion.5
  8.9 0.0 copy-done
  8.9 1.8 convolution_convert_fusion.3
  10.7 6.2 %convolution_convert_fusion.1 = bf16[4,64,64]{2,1,0:T(8,128)(2,1)S(1)} fusion(bf16[256,14336]{1,0:T(8,128)(2,1)} %param.6, bf16[14336,64]{0,1:T(8,128)(2,1)} %param.9, bf16[256,64]{0,1:T(8,128)(2,1)S(1)} %convolution_convert_fusion.3, bf16[4,256]{1,0:T(4,128)(2,1)S(1)} %fusion.5), kind=kOutput, calls=%fused_computation.1 | convolution fusion | flops 478248960 | bytes 9242624 | tf_op jit(solution)/shard_map/eti,tj->eij/dot_general | solution.py:24
  16.9 0.1 convert_element_type.26
  17.0 151.9 %all-gather.2.cloned.1.call-done = bf16[2048,4096]{1,0:T(8,128)(2,1)} async-done(((bf16[32,4096]{1,0:T(8,128)(2,1)}), bf16[2048,4096]{1,0:T(8,128)(2,1)}) %all-gather.2.cloned.1.call-update) | async-done | bytes 16777232 | tf_op jit(solution)/shard_map/all_gather | solution.py:29
  168.9 10.8 %convolution_convert_fusion = bf16[4,2048]{1,0:T(4,128)(2,1)} fusion(bf16[4,4096]{1,0:T(4,128)(2,1)S(1)} %convert_element_type.26, bf16[2048,4096]{1,0:T(8,128)(2,1)} %all-gather.2.cloned.1.call-done), kind=kOutput, calls=%fused_computation | convolution fusion | flops 67117056 | bytes 16826368 | tf_op jit(solution)/shard_map/dot_general | solution.py:27
Async XLA Ops:
  6.5 2.3 %copy-start = (bf16[256,4096]{1,0:T(8,128)(2,1)S(1)}, bf16[256,4096]{1,0:T(8,128)(2,1)}, u32[]{:S(2)}) copy-start(bf16[256,4096]{1,0:T(8,128)(2,1)} %param.7) | copy-start | bytes 6291460
  6.6 162.4 %all-gather.2.cloned.1.call-start = ((), (), s32[]{:S(2)}) async-start(), calls=%async_computation | async-start | bytes 17039360 | tf_op jit(solution)/shard_map/all_gather | solution.py:29
Sparse Core Ops, SparseCore 0:
  9.2 159.6 all-gather.1
where the time goes:
time: 188 us; the launch traced here: 187 us
  waiting for transfers between devices  153 us (81%)
  matrix products  18.8 us (10%)
  between operations  13.4 us (7%)
    all_gather x1, waiting for transfers between devices, local(): lax.all_gather(queries, 'dp', axis=0, tiled=True)  152 us
    dot_general x1, matrix products, local(): lax.dot_general(example_grads, lax.all_gather(queries, 'dp', axis=0, tile...  10.8 us
    dot_general x1, matrix products, local(): jnp.einsum('eti,tj->eij', masked_grads, proj_acts, preferred_element_type...  6.2 us
  transfers between devices with their start and end apart: 1, of which 1 were waited for; matrix products, arithmetic and copies ran while one was open for 5% of the time, Pallas kernels for 0%

commit v1 on v0

--- a/solution.py
+++ b/solution.py
@@ -14,23 +14,31 @@
         jnp.bfloat16
     )
     counts = lengths[0]
-    tok_ends = jnp.cumsum(counts)
-    tok_starts = tok_ends - counts
+    examples = counts.shape[0]
     position = jnp.arange(tok_count, dtype=jnp.int32)
-    member = (
-        (position[None, :] >= tok_starts[:, None]) & (position[None, :] < tok_ends[:, None])
-    ).astype(jnp.bfloat16)
-    masked_grads = member[:, :, None] * proj_grads[None, :, :]
-    summed = jnp.einsum("eti,tj->eij", masked_grads, proj_acts, preferred_element_type=jnp.float32)
-    example_grads = summed.reshape(counts.shape[0], rank_size * rank_size).astype(jnp.bfloat16)
+    tok_ends = [counts[0]]
+    for e in range(1, examples):
+        tok_ends.append(tok_ends[-1] + counts[e])
+    owner = sum((position >= end).astype(jnp.int32) for end in tok_ends[:-1])
+    member = (owner[:, None] == jnp.arange(examples)[None, :]).astype(jnp.bfloat16)
+    masked = (member[:, :, None] * proj_acts[:, None, :]).reshape(tok_count, examples * rank_size)
+    summed = lax.dot_general(
+        proj_grads, masked, (((0,), (0,)), ((), ())), preferred_element_type=jnp.float32
+    )
+    example_grads = (
+        summed.reshape(rank_size, examples, rank_size)
+        .transpose(1, 0, 2)
+        .reshape(examples, rank_size * rank_size)
+        .astype(jnp.bfloat16)
+    )
     contract = (((1,), (1,)), ((), ()))
     scores = lax.dot_general(
-        example_grads,
-        lax.all_gather(queries, "dp", axis=0, tiled=True),
+        lax.all_gather(example_grads, "dp", axis=0, tiled=True),
+        queries,
         contract,
         preferred_element_type=jnp.float32,
-    )
-    return scores.astype(jnp.bfloat16)
+    ).astype(jnp.bfloat16)
+    return lax.all_to_all(scores, "dp", split_axis=0, concat_axis=1, tiled=True)
 
 
 def solution(mesh):

time: 188 us -> 217 us (1.15)
  blocking collectives: 0 us -> 39.4 us
  matrix products: 18.8 us -> 9.29 us
  waiting for transfers between devices: 153 us -> 144 us
  local copies, waits for them, and re-layouts: 0.12 us -> 7.01 us
    all_to_all x0 -> x1, blocking collectives: none -> 39.4 us  [local(): return lax.all_to_all(scores, 'dp', split_axis=0, concat_axis=1, tiled=True)]
    dot_general x3, matrix products: 18.8 us -> 9.29 us  [the longest x1 5.99 us: local(): jnp.dot(activations, proj_in, preferred_element_type=jnp.float32)]
    all_gather x1, waiting for transfers between devices: 152 us -> 144 us  [local(): lax.all_gather(example_grads, 'dp', axis=0, tiled=True)]
    unnamed x2 -> x8, local copies, waits for them, and re-layouts: 0.01 us -> 4.71 us
  transfers between devices with their start and end apart: 1 -> 1, of which waited for: 1 -> 1; matrix products, arithmetic and copies ran while one was open for 5% -> 0% of each run, Pallas kernels for 0% -> 0%
where the time goes in v1:
time: 217 us; the launch traced here: 216 us
  waiting for transfers between devices  144 us (66%)
  blocking collectives  39.4 us (18%)
  between operations  15.4 us (7%)
  matrix products  9.29 us (4%)
  local copies, waits for them, and re-layouts  7.01 us (3%)
    all_gather x1, waiting for transfers between devices, local(): lax.all_gather(example_grads, 'dp', axis=0, tiled=True)  144 us
    all_to_all x1, blocking collectives, local(): return lax.all_to_all(scores, 'dp', split_axis=0, concat_axis=1, tiled=True)  39.4 us
    dot_general x1, matrix products, local(): jnp.dot(activations, proj_in, preferred_element_type=jnp.float32)  5.99 us
    unnamed x8, local copies, waits for them, and re-layouts  4.71 us
  transfers between devices with their start and end apart: 1, of which 1 were waited for; matrix products, arithmetic and copies ran while one was open for 0% of the time, Pallas kernels for 0%

profile of v1, /device:TPU:44, one launch (start us, length us, event | category | flops | bytes accessed | tf_op | source)
XLA Modules:
  0.0 215.6 jit_solution(11846224290307808529)
XLA Ops:
  6.5 0.0 copy-start
  6.6 0.0 all-gather.3.cloned.1.call-start
  6.6 1.4 fusion.9
  9.9 0.7 fusion.8
  10.6 0.0 copy-start.1
  10.6 6.0 %convolution_convert_fusion.1 = bf16[256,64]{0,1:T(8,128)(2,1)S(1)} fusion(bf16[256,14336]{1,0:T(8,128)(2,1)} %param.6, bf16[14336,64]{0,1:T(8,128)(2,1)} %param.9), kind=kOutput, calls=%fused_computation.2 | convolution fusion | flops 469778432 | bytes 9207808 | tf_op jit(solution)/shard_map/dot_general | solution.py:10
  16.6 0.0 copy-done
  16.6 0.0 copy-done.1
  16.6 1.0 fusion
  17.6 0.7 reshape.52
  18.3 0.1 all-gather.3.cloned.1.call-update
  18.4 0.0 copy-start.2
  18.4 143.7 %all-gather.3.cloned.1.call-done = bf16[64,4,4096]{2,1,0:T(4,128)(2,1)} async-done(((bf16[1,4,4096]{2,1,0:T(4,128)(2,1)}), bf16[64,4,4096]{2,1,0:T(4,128)(2,1)}) %all-gather.3.cloned.1.call-update) | async-done | bytes 2097168 | tf_op jit(solution)/shard_map/all_gather | solution.py:36
  162.2 4.0 %reshape.53 = bf16[256,4096]{1,0:T(8,128)(2,1)} reshape(bf16[64,4,4096]{2,1,0:T(4,128)(2,1)} %all-gather.3.cloned.1.call-done) | data formatting | bytes 4194304
  166.1 0.0 copy-done.2
  166.1 2.3 %convolution_convert_fusion.3 = bf16[256,32]{0,1:T(8,128)(2,1)S(1)} fusion(bf16[256,4096]{1,0:T(8,128)(2,1)} %reshape.53, bf16[32,4096]{1,0:T(8,128)(2,1)S(1)} %copy-done.2), kind=kOutput, calls=%fused_computation.5 | convolution fusion | flops 67117056 | bytes 2375680 | tf_op jit(solution)/shard_map/dot_general | solution.py:35
  168.4 0.1 copy.10
  168.6 39.4 %all_to_all.19 = bf16[64,4,32]{2,1,0:T(4,128)(2,1)S(1)} all-to-all(bf16[64,4,32]{2,1,0:T(4,128)(2,1)S(1)} %bitcast.24), channel_id=1, replica_groups=mesh['parts'=4,'dp'=64] {'dp'}, dimensions={0} | all-to-all | bytes 32768 | tf_op jit(solution)/shard_map/all_to_all | solution.py:41
  208.0 0.7 all_to_all.17
  (2 shorter events, 0.0 us)
Async XLA Ops:
  6.5 10.1 %copy-start = (bf16[256,4096]{1,0:T(8,128)(2,1)S(1)}, bf16[256,4096]{1,0:T(8,128)(2,1)}, u32[]{:S(2)}) copy-start(bf16[256,4096]{1,0:T(8,128)(2,1)} %param.7) | copy-start | bytes 6291460
  6.6 155.6 %all-gather.3.cloned.1.call-start = ((), (), s32[]{:S(2)}) async-start(), calls=%async_computation.1 | async-start | bytes 2129920 | tf_op jit(solution)/shard_map/all_gather | solution.py:36
  10.6 6.0 %copy-start.1 = (bf16[4096,64]{0,1:T(8,128)(2,1)S(1)}, bf16[4096,64]{0,1:T(8,128)(2,1)}, u32[]{:S(2)}) copy-start(bf16[4096,64]{0,1:T(8,128)(2,1)} %param.10) | copy-start | bytes 1572868
  18.4 147.7 %copy-start.2 = (bf16[32,4096]{1,0:T(8,128)(2,1)S(1)}, bf16[32,4096]{1,0:T(8,128)(2,1)}, u32[]{:S(2)}) copy-start(bf16[32,4096]{1,0:T(8,128)(2,1)} %param.11) | copy-start | bytes 786436
Sparse Core Ops, SparseCore 0:
  18.5 143.5 all-gather.2

commit v2 on v0

v2 whole, which is shorter than its diff:
```python
import functools

import jax
import jax.numpy as jnp
from jax import lax
from jax.experimental import pallas as pl
from jax.experimental.pallas import tpu as pltpu
from jax.sharding import PartitionSpec as P

MESH = pl.DeviceIdType.MESH
STRIDE = 4
F32 = jnp.float32
BF16 = jnp.bfloat16
NT = (((1,), (1,)), ((), ()))


def cuts(total, size):
    widths = [size] * (total // size)
    if total % size:
        widths.append(total % size)
    if widths[-1] % 256 == 0 and widths[-1] >= 512:
        widths[-1:] = [widths[-1] // 2] * 2
    starts = [sum(widths[:i]) for i in range(len(widths))]
    return list(zip(starts, widths))


def kernel(
    nz, chunk, acts, grads, lens, pin, pout, qs, out,
    abuf, gbuf, pinb, poutb, qv, qbuf, ybuf, rbuf, sbuf, res,
    loc_sem, qloc_sem, qsend, qrecv, dsend, fsend, erecv, rsend, rrecv,
):
    me = lax.axis_index("dp")
    z, core = me // 2, lax.rem(me, 2)
    part = lax.rem(z, STRIDE)
    groups = nz // (2 * STRIDE)
    blocks = 2 * STRIDE
    toks, ff = acts.shape
    d = grads.shape[1]
    rank = pin.shape[0]
    kq = qs.shape[1] // STRIDE

    def chip(dz):
        return lax.rem(z + nz + dz, nz)

    def dev(dz):
        return {"dp": chip(dz) * 2 + core}

    partner = {"dp": z * 2 + 1 - core}

    def remote(src, dst, ssem, rsem, to):
        return pltpu.make_async_remote_copy(
            src_ref=src, dst_ref=dst, send_sem=ssem, recv_sem=rsem,
            device_id=to, device_id_type=MESH,
        )

    barrier = pltpu.get_barrier_semaphore()
    near = [dz for t in range(1, STRIDE + 1) for dz in (t, -t)]
    for dz in near:
        pl.semaphore_signal(barrier, inc=1, device_id=dev(dz), device_id_type=MESH)
    pl.semaphore_signal(barrier, inc=1, device_id=partner, device_id_type=MESH)

    def q_cols(dz):
        return pl.ds(pl.multiple_of(lax.rem(z + nz + dz, STRIDE) * kq, kq), kq)

    q_all = pltpu.make_async_copy(qs, qv, qloc_sem.at[0])
    q_own = pltpu.make_async_copy(qs.at[:, q_cols(0)], qbuf.at[part * 2 + core], qloc_sem.at[1])
    q_all.start()
    q_own.start()
    n_sem = 0
    g_chunks, a_chunks = [], []
    pout_copy = pltpu.make_async_copy(pout, poutb, loc_sem.at[n_sem])
    pout_copy.start()
    n_sem += 1
    for lo, w in cuts(d, chunk):
        cp = pltpu.make_async_copy(
            grads.at[:, pl.ds(lo, w)], gbuf.at[:, pl.ds(lo, w)], loc_sem.at[n_sem]
        )
        cp.start()
        n_sem += 1
        g_chunks.append((lo, w, cp))
    for lo, w in cuts(ff, chunk):
        cp0 = pltpu.make_async_copy(
            pin.at[:, pl.ds(lo, w)], pinb.at[:, pl.ds(lo, w)], loc_sem.at[n_sem]
        )
        cp1 = pltpu.make_async_copy(
            acts.at[:, pl.ds(lo, w)], abuf.at[:, pl.ds(lo, w)], loc_sem.at[n_sem + 1]
        )
        cp0.start()
        cp1.start()
        n_sem += 2
        a_chunks.append((lo, w, cp0, cp1))

    pg = jnp.zeros((toks, rank), F32)
    pout_copy.wait()
    for lo, w, cp in g_chunks:
        cp.wait()
        pg = pg + lax.dot_general(
            gbuf[:, lo : lo + w], poutb[:, lo : lo + w], NT, preferred_element_type=F32
        )
    pg = pg.astype(BF16)
    rows = 4 * rank
    r = lax.broadcasted_iota(jnp.int32, (rows, rank), 0)
    i = lax.broadcasted_iota(jnp.int32, (rows, rank), 1)
    quarter = r // rank
    i_lo = (quarter & 1) * 2 + quarter // 2
    spread = (i == ((r & (rank - 1)) & ~3) + i_lo).astype(F32).astype(BF16)
    wide = lax.dot_general(spread, pg, NT, preferred_element_type=F32)
    e = lax.broadcasted_iota(jnp.int32, (rows, toks), 0) & 3
    tok = lax.broadcasted_iota(jnp.int32, (rows, toks), 1)
    end0 = lens[0, 0]
    end1 = end0 + lens[0, 1]
    end2 = end1 + lens[0, 2]
    owner = (
        (tok >= end0).astype(jnp.int32)
        + (tok >= end1).astype(jnp.int32)
        + (tok >= end2).astype(jnp.int32)
    )
    lhs = jnp.where(owner == e, wide, 0.0).astype(BF16)

    pa = jnp.zeros((toks, 2 * rank), F32)
    q_sends = []
    for n, (lo, w, cp0, cp1) in enumerate(a_chunks):
        if n == len(a_chunks) // 2:
            q_all.wait()
            pl.semaphore_wait(barrier, len(near) + 1)
            slot = part * 2 + core
            for k, dz in enumerate((1, -1)):
                q_sends.append(
                    remote(qv.at[:, q_cols(dz)], qbuf.at[slot], qsend.at[k], qrecv.at[k], dev(dz))
                )
            far = {"dp": lax.rem(z + nz + 2 - 4 * core, nz) * 2 + core}
            q_sends.append(
                remote(qv.at[:, q_cols(2)], qbuf.at[slot], qsend.at[2], qrecv.at[2], far)
            )
            q_sends.append(
                remote(qv.at[:, q_cols(0)], qbuf.at[slot], qsend.at[3], qrecv.at[3], partner)
            )
            for cp in q_sends:
                cp.start()
        cp0.wait()
        cp1.wait()
        p = pinb[:, lo : lo + w]
        pa = pa + lax.dot_general(
            abuf[:, lo : lo + w], jnp.concatenate([p, p], axis=0), NT, preferred_element_type=F32
        )
    left = lax.broadcasted_iota(jnp.int32, (toks, 2 * rank), 1) < rank
    pa_l = jnp.where(left, pa, 0.0).astype(BF16)
    pa_r = jnp.where(left, 0.0, pa).astype(BF16)
    half = 2 * rank
    y = jnp.dot(lhs[:half], pa_l, preferred_element_type=F32) + jnp.dot(
        lhs[half:], pa_r, preferred_element_type=F32
    )
    y = jnp.concatenate([y[:rank], y[rank:]], axis=1).astype(BF16)
    own_rows = rank // STRIDE
    for s in range(STRIDE):
        ybuf[s] = y[s * own_rows : (s + 1) * own_rows]

    def slot_of(m, direction, t):
        return m * blocks + direction * STRIDE + t - 1

    last = groups * blocks - 1
    direct = []
    for t in range(STRIDE, 0, -1):
        for direction in (0, 1):
            k = slot_of(0, direction, t)
            if k == last:
                continue
            dz = t if direction == 0 else -t
            direct.append(
                remote(
                    ybuf.at[lax.rem(z + nz + dz, STRIDE)], rbuf.at[k],
                    dsend.at[k], erecv.at[k], dev(dz),
                )
            )
            direct[-1].start()
    rbuf[last] = ybuf[part]

    q_own.wait()
    passed = []
    for k in range(3):
        if k == 0:
            from_slot = lax.rem(z + nz - 1, STRIDE) * 2 + core
        elif k == 1:
            from_slot = lax.rem(z + 1, STRIDE) * 2 + core
        else:
            from_slot = lax.rem(z + 2, STRIDE) * 2 + core
        q_sends[k].wait_recv()
        passed.append(
            remote(
                qbuf.at[from_slot], qbuf.at[from_slot], qsend.at[4 + k], qrecv.at[4 + k], partner
            )
        )
        passed[-1].start()

    def arrival(k):
        return remote(rbuf.at[k], rbuf.at[k], fsend.at[k], erecv.at[k], dev(STRIDE))

    forwards, returns = [], []
    sub = lax.broadcasted_iota(jnp.int32, (blocks, 8, 128), 1) < 4
    for m in range(groups):
        for t in range(STRIDE, 0, -1):
            for direction in (0, 1):
                k = slot_of(m, direction, t)
                if k == last:
                    continue
                arrival(k).wait_recv()
                nxt = k + blocks
                if nxt < groups * blocks and nxt != last:
                    fw = remote(
                        rbuf.at[k], rbuf.at[nxt], fsend.at[k], erecv.at[nxt],
                        dev(STRIDE if direction == 0 else -STRIDE),
                    )
                    fw.start()
                    forwards.append(fw)
        if m == 0:
            q_sends[3].wait_recv()
            for cp in passed:
                cp.wait_recv()
        held = rbuf[m * blocks : (m + 1) * blocks].reshape(blocks * own_rows, 4 * rank)
        prods = []
        for g in range(STRIDE):
            w = qbuf[:, :, g * 256 : (g + 1) * 256].reshape(-1, 256)
            pr = lax.dot_general(held, w, NT, preferred_element_type=F32)
            pr = pr.reshape(blocks, own_rows, pr.shape[-1])
            prods.append(pr[:, 8 * (g // 2) : 8 * (g // 2) + 8])
        packed = []
        for h in range(2):
            c0, c1 = h * 128, (h + 1) * 128
            s = jnp.where(sub, prods[0][:, :, c0:c1], prods[1][:, :, c0:c1])
            s = s + jnp.where(sub, prods[2][:, :, c0:c1], prods[3][:, :, c0:c1])
            packed.append(s + pltpu.roll(s, 4, 1))
        sbuf[m * blocks : (m + 1) * blocks] = jnp.where(sub, packed[0], packed[1]).astype(BF16)
        for t in range(STRIDE, 0, -1):
            for direction in (0, 1):
                k = slot_of(m, direction, t)
                if k == last:
                    continue
                dist = m * STRIDE + t
                back = remote(
                    sbuf.at[k], res.at[z], rsend.at[k], rrecv.at[z],
                    dev(-dist if direction == 0 else dist),
                )
                back.start()
                returns.append(back)
    res[z] = sbuf[last]

    for dz in range(1, nz):
        src = chip(dz)
        remote(res.at[src], res.at[src], rsend.at[0], rrecv.at[src], partner).wait_recv()

    row = lax.broadcasted_iota(jnp.int32, (8, 128), 0)
    lane = lax.broadcasted_iota(jnp.int32, (8, 128), 1)
    col = (row // 4) * 128 + lane
    segments = nz // STRIDE
    acc = [jnp.zeros((8, 128), F32) for _ in range(segments)]
    for rho in range(STRIDE):
        gap = (col // 64 - rho + STRIDE) & (STRIDE - 1)
        shift = jnp.where(gap == 3, -1, gap)
        shift = jnp.where(gap == 2, jnp.where((col // 32) % 2 == 0, -2, 2), shift)
        target = rho + shift
        seg_masks = {-1: target < 0, 0: (target >= 0) & (target < STRIDE), 1: target >= STRIDE}
        used = {0} | ({-1} if rho < 2 else set()) | ({1} if rho >= STRIDE - 2 else set())
        for s in range(segments):
            val = res[s * STRIDE + rho].astype(F32)
            for rel in sorted(used):
                to = (s + rel) % segments
                acc[to] = acc[to] + jnp.where(seg_masks[rel], val, 0.0)
    for s in range(segments):
        out[:, s * 256 : s * 256 + 128] = acc[s][:4].astype(out.dtype)
        out[:, s * 256 + 128 : s * 256 + 256] = acc[s][4:].astype(out.dtype)

    for cp in q_sends + passed + direct + forwards + returns:
        cp.wait_send()


def local(nz, activations, out_grads, lengths, proj_in, proj_out, queries):
    toks, ff = activations.shape
    d = out_grads.shape[1]
    rank = proj_in.shape[1]
    nq, params = queries.shape
    chunk = min(2048, d)
    n_loc = 1 + len(cuts(d, chunk)) + 2 * len(cuts(ff, chunk))
    dma = pltpu.SemaphoreType.DMA
    anyspec = pl.BlockSpec(memory_space=pl.ANY)
    rows = rank // STRIDE
    return pl.pallas_call(
        functools.partial(kernel, nz, chunk),
        out_shape=jax.ShapeDtypeStruct((lengths.shape[1], 2 * nz * nq), BF16),
        in_specs=[
            anyspec, anyspec, pl.BlockSpec(memory_space=pltpu.SMEM), anyspec, anyspec, anyspec,
        ],
        out_specs=pl.BlockSpec(memory_space=pltpu.VMEM),
        scratch_shapes=[
            pltpu.VMEM((toks, ff), BF16),
            pltpu.VMEM((toks, d), BF16),
            pltpu.VMEM((rank, ff), BF16),
            pltpu.VMEM((rank, d), BF16),
            pltpu.VMEM((nq, params), BF16),
            pltpu.VMEM((2 * STRIDE, nq, params // STRIDE), BF16),
            pltpu.VMEM((STRIDE, rows, 4 * rank), BF16),
            pltpu.VMEM((nz, rows, 4 * rank), BF16),
            pltpu.VMEM((nz, 8, 128), BF16),
            pltpu.VMEM((nz, 8, 128), BF16),
            dma((n_loc,)), dma((2,)), dma((7,)), dma((7,)), dma((2 * STRIDE,)),
            dma((nz,)), dma((nz,)), dma((nz,)), dma((nz,)),
        ],
        compiler_params=pltpu.CompilerParams(collective_id=0, has_side_effects=True),
        name="score",
    )(activations, out_grads, lengths, proj_in.T, proj_out.T, queries)


def solution(mesh):
    both = P(("parts", "dp"), None)
    in_specs = (both, both, both, P(), P(), both)
    body = functools.partial(local, mesh.shape["dp"] // 2)
    return jax.shard_map(body, mesh=mesh, in_specs=in_specs, out_specs=both, check_vma=False)
```

time: 188 us -> 67.4 us (0.36)
  waiting for transfers between devices: 153 us -> 0 us
  Pallas kernels: 0 us -> 65.9 us
  matrix products: 18.8 us -> 0 us
  between operations: 13.4 us -> 0.01 us
    all_gather x1 -> x0, waiting for transfers between devices: 152 us -> none  [local(): lax.all_gather(queries, 'dp', axis=0, tiled=True)]
    pallas_call x0 -> x1, Pallas kernels: none -> 65.9 us  [local(): pl.pallas_call(functools.partial(kernel, nz, chunk), out_shape=jax.ShapeD...]
    dot_general x3 -> x0, matrix products: 18.8 us -> none  [the longest x1 10.8 us: local(): lax.dot_general(example_grads, lax.all_gather(queries, 'dp', axis=0, tile...]
  transfers between devices with their start and end apart: 1 -> 0, of which waited for: 1 -> 0; matrix products, arithmetic and copies ran while one was open for 5% -> 0% of each run, Pallas kernels for 0% -> 0%
where the time goes in v2:
time: 67.4 us; the launch traced here: 67.3 us
  Pallas kernels  65.9 us (98%)
  local copies, waits for them, and re-layouts  1.33 us (2%)
    pallas_call x1, Pallas kernels, local(): pl.pallas_call(functools.partial(kernel, nz, chunk), out_shape=jax.ShapeD...  65.9 us

profile of v2, /device:TPU:44, one launch (start us, length us, event | category | flops | bytes accessed | tf_op | source)
XLA Modules:
  0.0 67.3 jit_solution(17670830792612829153)
XLA Ops:
  0.0 65.9 %score.1 = bf16[4,2048]{1,0:T(4,128)(2,1)} custom-call(bf16[256,14336]{1,0:T(8,128)(2,1)} %acts.1, bf16[256,4096]{1,0:T(8,128)(2,1)} %grads.1, s32[1,4]{1,0:T(1,128)} %lens.1, bf16[64,14336]{1,0:T(8,128)(2,1)} %bitcast.2, bf16[64,4096]{1,0:T(8,128)(2,1)} %bitcast.3, bf16[32,4096]{1,0:T(8,128)(2,1)} %qs.1), custom_call_target="tpu_custom_call" | custom-call | tf_op jit(solution)/shard_map/score/pallas_call | solution.py:286
  65.9 1.3 %copy.8 = bf16[4,2048]{1,0:T(4,128)(2,1)} copy(bf16[4,2048]{1,0:T(4,128)(2,1)} %score.1) | data formatting | bytes 32768

commit v3 on v2

--- a/solution.py
+++ b/solution.py
@@ -24,15 +24,21 @@
     return list(zip(starts, widths))
 
 
+def split(nz):
+    total = nz // STRIDE
+    up = max(total * 5 // 8, total // 2)
+    return up, total - up
+
+
 def kernel(
     nz, chunk, acts, grads, lens, pin, pout, qs, out,
     abuf, gbuf, pinb, poutb, qv, qbuf, ybuf, rbuf, sbuf, res,
-    loc_sem, qloc_sem, qsend, qrecv, dsend, fsend, erecv, rsend, rrecv,
+    loc_sem, qloc_sem, qsend, qrecv, dsend, fsend, erecv, rsend, rrecv, wrap_sem,
 ):
     me = lax.axis_index("dp")
     z, core = me // 2, lax.rem(me, 2)
     part = lax.rem(z, STRIDE)
-    groups = nz // (2 * STRIDE)
+    r_groups, l_groups = split(nz)
     blocks = 2 * STRIDE
     toks, ff = acts.shape
     d = grads.shape[1]
@@ -55,9 +61,21 @@
 
     barrier = pltpu.get_barrier_semaphore()
     near = [dz for t in range(1, STRIDE + 1) for dz in (t, -t)]
+
+    def greet(sem, dz):
+        pl.semaphore_signal(sem, inc=1, device_id=dev(dz), device_id_type=MESH)
+
     for dz in near:
-        pl.semaphore_signal(barrier, inc=1, device_id=dev(dz), device_id_type=MESH)
+        if dz < 0:
+            greet(barrier, dz)
+        else:
+            pl.when(z + dz < nz)(functools.partial(greet, barrier, dz))
     pl.semaphore_signal(barrier, inc=1, device_id=partner, device_id_type=MESH)
+
+    def await_near():
+        pl.semaphore_wait(barrier, len(near) + 1 - jnp.maximum(STRIDE - z, 0))
+        for dz in range(1, STRIDE + 1):
+            pl.when(z + dz >= nz)(functools.partial(greet, wrap_sem, dz))
 
     def q_cols(dz):
         return pl.ds(pl.multiple_of(lax.rem(z + nz + dz, STRIDE) * kq, kq), kq)
@@ -118,25 +136,21 @@
     lhs = jnp.where(owner == e, wide, 0.0).astype(BF16)
 
     pa = jnp.zeros((toks, 2 * rank), F32)
-    q_sends = []
+    slot = part * 2 + core
+    q_up = remote(qv.at[:, q_cols(1)], qbuf.at[slot], qsend.at[0], qrecv.at[0], dev(1))
+    q_down = remote(qv.at[:, q_cols(-1)], qbuf.at[slot], qsend.at[1], qrecv.at[1], dev(-1))
+    far = {"dp": lax.rem(z + nz + 2 - 4 * core, nz) * 2 + core}
+    q_far = remote(qv.at[:, q_cols(2)], qbuf.at[slot], qsend.at[2], qrecv.at[2], far)
+    q_near = remote(qv.at[:, q_cols(0)], qbuf.at[slot], qsend.at[3], qrecv.at[3], partner)
+    q_sends = [q_up, q_down, q_far, q_near]
     for n, (lo, w, cp0, cp1) in enumerate(a_chunks):
         if n == len(a_chunks) // 2:
             q_all.wait()
-            pl.semaphore_wait(barrier, len(near) + 1)
-            slot = part * 2 + core
-            for k, dz in enumerate((1, -1)):
-                q_sends.append(
-                    remote(qv.at[:, q_cols(dz)], qbuf.at[slot], qsend.at[k], qrecv.at[k], dev(dz))
-                )
-            far = {"dp": lax.rem(z + nz + 2 - 4 * core, nz) * 2 + core}
-            q_sends.append(
-                remote(qv.at[:, q_cols(2)], qbuf.at[slot], qsend.at[2], qrecv.at[2], far)
-            )
-            q_sends.append(
-                remote(qv.at[:, q_cols(0)], qbuf.at[slot], qsend.at[3], qrecv.at[3], partner)
-            )
-            for cp in q_sends:
-                cp.start()
+            await_near()
+            q_up.start()
+            q_near.start()
+            pl.when((z >= STRIDE) | (core == 0))(q_far.start)
+            pl.when(z >= STRIDE)(q_down.start)
         cp0.wait()
         cp1.wait()
         p = pinb[:, lo : lo + w]
@@ -155,93 +169,105 @@
     for s in range(STRIDE):
         ybuf[s] = y[s * own_rows : (s + 1) * own_rows]
 
-    def slot_of(m, direction, t):
-        return m * blocks + direction * STRIDE + t - 1
-
-    last = groups * blocks - 1
-    direct = []
-    for t in range(STRIDE, 0, -1):
-        for direction in (0, 1):
-            k = slot_of(0, direction, t)
-            if k == last:
-                continue
-            dz = t if direction == 0 else -t
-            direct.append(
-                remote(
-                    ybuf.at[lax.rem(z + nz + dz, STRIDE)], rbuf.at[k],
-                    dsend.at[k], erecv.at[k], dev(dz),
+    def base(m):
+        return m * blocks if m < l_groups else l_groups * blocks + (m - l_groups) * STRIDE
+
+    def slot_of(m, up, t):
+        return base(m) + (0 if up else STRIDE) + t - 1
+
+    last = slot_of(l_groups - 1, False, STRIDE)
+
+    def leg(up, t):
+        k = slot_of(0, up, t)
+        dz = t if up else -t
+        return remote(
+            ybuf.at[lax.rem(z + nz + dz, STRIDE)], rbuf.at[k], dsend.at[k], erecv.at[k], dev(dz)
+        )
+
+    hops = range(STRIDE, 0, -1)
+    ups = [leg(True, t) for t in hops]
+    downs = [leg(False, t) for t in hops if slot_of(0, False, t) != last]
+    for cp in ups:
+        cp.start()
+
+    def start_downs():
+        for cp in downs:
+            cp.start()
+
+    def after_wrap():
+        pl.semaphore_wait(wrap_sem, STRIDE - z)
+        q_down.start()
+        pl.when(core == 1)(q_far.start)
+        start_downs()
+
+    pl.when(z >= STRIDE)(start_downs)
+    rbuf[last] = ybuf[part]
+    q_own.wait()
+
+    forwards, returns, passed = [], [], []
+
+    def pass_on(k, up, nxt):
+        remote(rbuf.at[k], rbuf.at[k], fsend.at[k], erecv.at[k], dev(STRIDE)).wait_recv()
+        if nxt is not None and nxt != last:
+            fw = remote(
+                rbuf.at[k], rbuf.at[nxt], fsend.at[k], erecv.at[nxt], dev(STRIDE if up else -STRIDE)
+            )
+            fw.start()
+            forwards.append(fw)
+
+    def returning(k, dist):
+        back = remote(sbuf.at[k], res.at[z], rsend.at[k], rrecv.at[z], dev(dist))
+        back.start()
+        returns.append(back)
+
+    for m in range(r_groups):
+        for t in range(1, STRIDE + 1):
+            if m == 0:
+                pl.when(z == t - 1)(after_wrap)
+            pass_on(
+                slot_of(m, True, t), True, slot_of(m + 1, True, t) if m + 1 < r_groups else None
+            )
+        if m == 0:
+            for k, dz in enumerate((-1, 1, 2)):
+                came = lax.rem(z + nz + dz, STRIDE) * 2 + core
+                q_sends[k].wait_recv()
+                passed.append(
+                    remote(
+                        qbuf.at[came], qbuf.at[came], qsend.at[4 + k], qrecv.at[4 + k], partner
+                    )
                 )
-            )
-            direct[-1].start()
-    rbuf[last] = ybuf[part]
-
-    q_own.wait()
-    passed = []
-    for k in range(3):
-        if k == 0:
-            from_slot = lax.rem(z + nz - 1, STRIDE) * 2 + core
-        elif k == 1:
-            from_slot = lax.rem(z + 1, STRIDE) * 2 + core
-        else:
-            from_slot = lax.rem(z + 2, STRIDE) * 2 + core
-        q_sends[k].wait_recv()
-        passed.append(
-            remote(
-                qbuf.at[from_slot], qbuf.at[from_slot], qsend.at[4 + k], qrecv.at[4 + k], partner
-            )
-        )
-        passed[-1].start()
-
-    def arrival(k):
-        return remote(rbuf.at[k], rbuf.at[k], fsend.at[k], erecv.at[k], dev(STRIDE))
-
-    forwards, returns = [], []
-    sub = lax.broadcasted_iota(jnp.int32, (blocks, 8, 128), 1) < 4
-    for m in range(groups):
-        for t in range(STRIDE, 0, -1):
-            for direction in (0, 1):
-                k = slot_of(m, direction, t)
-                if k == last:
-                    continue
-                arrival(k).wait_recv()
-                nxt = k + blocks
-                if nxt < groups * blocks and nxt != last:
-                    fw = remote(
-                        rbuf.at[k], rbuf.at[nxt], fsend.at[k], erecv.at[nxt],
-                        dev(STRIDE if direction == 0 else -STRIDE),
+                passed[-1].start()
+        if m < l_groups:
+            for t in range(1, STRIDE + 1):
+                if slot_of(m, False, t) != last:
+                    pass_on(
+                        slot_of(m, False, t), False,
+                        slot_of(m + 1, False, t) if m + 1 < l_groups else None,
                     )
-                    fw.start()
-                    forwards.append(fw)
         if m == 0:
-            q_sends[3].wait_recv()
+            q_near.wait_recv()
             for cp in passed:
                 cp.wait_recv()
-        held = rbuf[m * blocks : (m + 1) * blocks].reshape(blocks * own_rows, 4 * rank)
+        count = blocks if m < l_groups else STRIDE
+        held = rbuf[base(m) : base(m) + count].reshape(count * own_rows, 4 * rank)
         prods = []
         for g in range(STRIDE):
             w = qbuf[:, :, g * 256 : (g + 1) * 256].reshape(-1, 256)
             pr = lax.dot_general(held, w, NT, preferred_element_type=F32)
-            pr = pr.reshape(blocks, own_rows, pr.shape[-1])
+            pr = pr.reshape(count, own_rows, pr.shape[-1])
             prods.append(pr[:, 8 * (g // 2) : 8 * (g // 2) + 8])
+        sub = lax.broadcasted_iota(jnp.int32, (count, 8, 128), 1) < 4
         packed = []
         for h in range(2):
             c0, c1 = h * 128, (h + 1) * 128
             s = jnp.where(sub, prods[0][:, :, c0:c1], prods[1][:, :, c0:c1])
             s = s + jnp.where(sub, prods[2][:, :, c0:c1], prods[3][:, :, c0:c1])
             packed.append(s + pltpu.roll(s, 4, 1))
-        sbuf[m * blocks : (m + 1) * blocks] = jnp.where(sub, packed[0], packed[1]).astype(BF16)
+        sbuf[base(m) : base(m) + count] = jnp.where(sub, packed[0], packed[1]).astype(BF16)
         for t in range(STRIDE, 0, -1):
-            for direction in (0, 1):
-                k = slot_of(m, direction, t)
-                if k == last:
-                    continue
-                dist = m * STRIDE + t
-                back = remote(
-                    sbuf.at[k], res.at[z], rsend.at[k], rrecv.at[z],
-                    dev(-dist if direction == 0 else dist),
-                )
-                back.start()
-                returns.append(back)
+            returning(slot_of(m, True, t), -(m * STRIDE + t))
+            if m < l_groups and slot_of(m, False, t) != last:
+                returning(slot_of(m, False, t), m * STRIDE + t)
     res[z] = sbuf[last]
 
     for dz in range(1, nz):
@@ -269,7 +295,7 @@
         out[:, s * 256 : s * 256 + 128] = acc[s][:4].astype(out.dtype)
         out[:, s * 256 + 128 : s * 256 + 256] = acc[s][4:].astype(out.dtype)
 
-    for cp in q_sends + passed + direct + forwards + returns:
+    for cp in q_sends + passed + ups + downs + forwards + returns:
         cp.wait_send()
 
 
@@ -302,7 +328,7 @@
             pltpu.VMEM((nz, 8, 128), BF16),
             pltpu.VMEM((nz, 8, 128), BF16),
             dma((n_loc,)), dma((2,)), dma((7,)), dma((7,)), dma((2 * STRIDE,)),
-            dma((nz,)), dma((nz,)), dma((nz,)), dma((nz,)),
+            dma((nz,)), dma((nz,)), dma((nz,)), dma((nz,)), pltpu.SemaphoreType.REGULAR,
         ],
         compiler_params=pltpu.CompilerParams(collective_id=0, has_side_effects=True),
         name="score",

time: 67.4 us -> 69.7 us (1.034)
  Pallas kernels: 65.9 us -> 67.9 us
    pallas_call x1, Pallas kernels: 65.9 us -> 67.9 us  [local(): pl.pallas_call(functools.partial(kernel, nz, chunk), out_shape=jax.ShapeD...]
where the time goes in v3:
time: 69.7 us; the launch traced here: 69.3 us
  Pallas kernels  67.9 us (97%)
  local copies, waits for them, and re-layouts  1.33 us (2%)
    pallas_call x1, Pallas kernels, local(): pl.pallas_call(functools.partial(kernel, nz, chunk), out_shape=jax.ShapeD...  67.9 us

profile of v3, /device:TPU:44, one launch (start us, length us, event | category | flops | bytes accessed | tf_op | source)
XLA Modules:
  0.0 69.3 jit_solution(11226797156085110433)
XLA Ops:
  0.0 67.9 %score.1 = bf16[4,2048]{1,0:T(4,128)(2,1)} custom-call(bf16[256,14336]{1,0:T(8,128)(2,1)} %acts.1, bf16[256,4096]{1,0:T(8,128)(2,1)} %grads.1, s32[1,4]{1,0:T(1,128)} %lens.1, bf16[64,14336]{1,0:T(8,128)(2,1)} %bitcast.2, bf16[64,4096]{1,0:T(8,128)(2,1)} %bitcast.3, bf16[32,4096]{1,0:T(8,128)(2,1)} %qs.1), custom_call_target="tpu_custom_call" | custom-call | tf_op jit(solution)/shard_map/score/pallas_call | solution.py:312
  67.9 1.3 %copy.8 = bf16[4,2048]{1,0:T(4,128)(2,1)} copy(bf16[4,2048]{1,0:T(4,128)(2,1)} %score.1) | data formatting | bytes 32768

commit v4 on v3

v4 whole, which is shorter than its diff:
```python
import functools

import jax
import jax.numpy as jnp
from jax import lax
from jax.experimental import pallas as pl
from jax.experimental.pallas import tpu as pltpu
from jax.sharding import PartitionSpec as P

MESH = pl.DeviceIdType.MESH
STRIDE = 4
F32 = jnp.float32
BF16 = jnp.bfloat16
NT = (((1,), (1,)), ((), ()))


def cuts(total, size):
    widths = [size] * (total // size)
    if total % size:
        widths.append(total % size)
    if widths[-1] % 256 == 0 and widths[-1] >= 512:
        widths[-1:] = [widths[-1] // 2] * 2
    starts = [sum(widths[:i]) for i in range(len(widths))]
    return list(zip(starts, widths))


def split(nz):
    total = nz // STRIDE
    return total - total // 2, total // 2


def kernel(
    nz, chunk, acts, grads, lens, pin, pout, qs, out,
    abuf, gbuf, pinb, poutb, qv, qbuf, ybuf, rbuf, sbuf, res,
    loc_sem, qloc_sem, qsend, qrecv, dsend, fsend, erecv, rsend, rrecv, wrap_sem, pg_sum, pa_sum,
):
    me = lax.axis_index("dp")
    z, core = me // 2, lax.rem(me, 2)
    part = lax.rem(z, STRIDE)
    r_groups, l_groups = split(nz)
    toks, ff = acts.shape
    d = grads.shape[1]
    rank = pin.shape[0]
    kq = qs.shape[1] // STRIDE

    def chip(dz):
        return lax.rem(z + nz + dz, nz)

    def dev(dz):
        return {"dp": chip(dz) * 2 + core}

    partner = {"dp": z * 2 + 1 - core}

    def remote(src, dst, ssem, rsem, to):
        return pltpu.make_async_remote_copy(
            src_ref=src, dst_ref=dst, send_sem=ssem, recv_sem=rsem,
            device_id=to, device_id_type=MESH,
        )

    def q_cols(dz):
        return pl.ds(pl.multiple_of(lax.rem(z + nz + dz, STRIDE) * kq, kq), kq)

    n_sem = 0
    g_chunks, a_chunks = [], []
    pout_copy = pltpu.make_async_copy(pout, poutb, loc_sem.at[n_sem])
    pout_copy.start()
    n_sem += 1
    for lo, w in cuts(d, chunk):
        cp = pltpu.make_async_copy(
            grads.at[:, pl.ds(lo, w)], gbuf.at[:, pl.ds(lo, w)], loc_sem.at[n_sem]
        )
        cp.start()
        n_sem += 1
        g_chunks.append((lo, w, cp))
    q_all = pltpu.make_async_copy(qs, qv, qloc_sem.at[0])
    q_own = pltpu.make_async_copy(qs.at[:, q_cols(0)], qbuf.at[part * 2 + core], qloc_sem.at[1])
    q_all.start()
    q_own.start()
    for lo, w in cuts(ff, chunk):
        cp0 = pltpu.make_async_copy(
            pin.at[:, pl.ds(lo, w)], pinb.at[:, pl.ds(lo, w)], loc_sem.at[n_sem]
        )
        cp1 = pltpu.make_async_copy(
            acts.at[:, pl.ds(lo, w)], abuf.at[:, pl.ds(lo, w)], loc_sem.at[n_sem + 1]
        )
        cp0.start()
        cp1.start()
        n_sem += 2
        a_chunks.append((lo, w, cp0, cp1))

    barrier = pltpu.get_barrier_semaphore()
    near = [dz for t in range(1, STRIDE + 1) for dz in (t, -t)]

    def greet(sem, dz):
        pl.semaphore_signal(sem, inc=1, device_id=dev(dz), device_id_type=MESH)

    for dz in near:
        if dz < 0:
            greet(barrier, dz)
        else:
            pl.when(z + dz < nz)(functools.partial(greet, barrier, dz))
    pl.semaphore_signal(barrier, inc=1, device_id=partner, device_id_type=MESH)

    def await_near():
        pl.semaphore_wait(barrier, len(near) + 1 - jnp.maximum(STRIDE - z, 0))
        for dz in range(1, STRIDE + 1):
            pl.when(z + dz >= nz)(functools.partial(greet, wrap_sem, dz))

    def add_product(x_ref, w_ref, lo, w, total, copies):
        for i in range(2):
            cols = slice(lo + i * (w // 2), lo + (i + 1) * (w // 2))
            p = w_ref[:, cols]
            p = jnp.concatenate([p] * copies, axis=0) if copies > 1 else p
            prod = lax.dot_general(x_ref[:, cols], p, NT, preferred_element_type=F32)
            width = prod.shape[1]
            if lo == 0:
                total[i, :, :width] = prod
            else:
                total[i, :, :width] += prod

    pout_copy.wait()
    for lo, w, cp in g_chunks:
        cp.wait()
        add_product(gbuf, poutb, lo, w, pg_sum, 1)
    pg = (pg_sum[0, :, :rank] + pg_sum[1, :, :rank]).astype(BF16)
    rows = 4 * rank
    r = lax.broadcasted_iota(jnp.int32, (rows, rank), 0)
    i = lax.broadcasted_iota(jnp.int32, (rows, rank), 1)
    quarter = r // rank
    i_lo = (quarter & 1) * 2 + quarter // 2
    spread = (i == ((r & (rank - 1)) & ~3) + i_lo).astype(F32).astype(BF16)
    wide = lax.dot_general(spread, pg, NT, preferred_element_type=F32)
    e = lax.broadcasted_iota(jnp.int32, (8, toks), 0) & 3
    tok = lax.broadcasted_iota(jnp.int32, (8, toks), 1)
    end0 = lens[0, 0]
    end1 = end0 + lens[0, 1]
    end2 = end1 + lens[0, 2]
    owner = (
        (tok >= end0).astype(jnp.int32)
        + (tok >= end1).astype(jnp.int32)
        + (tok >= end2).astype(jnp.int32)
    )
    member = (owner == e)[None]
    lhs = jnp.where(member, wide.reshape(rows // 8, 8, toks), 0.0).reshape(rows, toks).astype(BF16)

    slot = part * 2 + core
    q_up = remote(qv.at[:, q_cols(1)], qbuf.at[slot], qsend.at[0], qrecv.at[0], dev(1))
    q_down = remote(qv.at[:, q_cols(-1)], qbuf.at[slot], qsend.at[1], qrecv.at[1], dev(-1))
    far = {"dp": lax.rem(z + nz + 2 - 4 * core, nz) * 2 + core}
    q_far = remote(qv.at[:, q_cols(2)], qbuf.at[slot], qsend.at[2], qrecv.at[2], far)
    q_near = remote(qv.at[:, q_cols(0)], qbuf.at[slot], qsend.at[3], qrecv.at[3], partner)
    q_sends = [q_up, q_down, q_far, q_near]
    for n, (lo, w, cp0, cp1) in enumerate(a_chunks):
        if n == min(2, len(a_chunks) - 1):
            q_all.wait()
            await_near()
            q_up.start()
            q_near.start()
            pl.when((z >= STRIDE) | (core == 0))(q_far.start)
            pl.when(z >= STRIDE)(q_down.start)
        cp0.wait()
        cp1.wait()
        add_product(abuf, pinb, lo, w, pa_sum, 2)
    pa = pa_sum[0] + pa_sum[1]
    left = lax.broadcasted_iota(jnp.int32, (toks, 2 * rank), 1) < rank
    pa_l = jnp.where(left, pa, 0.0).astype(BF16)
    pa_r = jnp.where(left, 0.0, pa).astype(BF16)
    half = 2 * rank
    y = jnp.dot(lhs[:half], pa_l, preferred_element_type=F32) + jnp.dot(
        lhs[half:], pa_r, preferred_element_type=F32
    )
    y = jnp.concatenate([y[:rank], y[rank:]], axis=1).astype(BF16)
    own_rows = rank // STRIDE
    for s in range(STRIDE):
        ybuf[s] = y[s * own_rows : (s + 1) * own_rows]

    quads = nz // STRIDE
    quad = z // STRIDE

    def slot_of(source):
        return lax.rem(quad + quads - source // STRIDE, quads) * STRIDE + lax.rem(source, STRIDE)

    def leg(up, t):
        dz = t if up else -t
        k = lax.rem(chip(dz) // STRIDE + quads - quad, quads) * STRIDE + part
        i = (0 if up else STRIDE) + t - 1
        return remote(
            ybuf.at[lax.rem(z + nz + dz, STRIDE)], rbuf.at[k], dsend.at[i], erecv.at[k], dev(dz)
        )

    hops = range(STRIDE, 0, -1)
    ups = [leg(True, t) for t in hops]
    downs = [leg(False, t) for t in hops if l_groups > 1 or t < STRIDE]
    for cp in ups:
        cp.start()

    def start_downs():
        for cp in downs:
            cp.start()

    def after_wrap():
        pl.semaphore_wait(wrap_sem, STRIDE - z)
        q_down.start()
        pl.when(core == 1)(q_far.start)
        start_downs()

    pl.when(z >= STRIDE)(start_downs)
    rbuf[part] = ybuf[part]
    q_own.wait()

    up_reach, down_reach = r_groups * STRIDE, l_groups * STRIDE - 1

    def onward(k, up):
        nxt = lax.rem(k + (STRIDE if up else nz - STRIDE), nz)
        return remote(
            rbuf.at[k], rbuf.at[nxt], fsend.at[k], erecv.at[nxt], dev(STRIDE if up else -STRIDE)
        )

    def take(i, up):
        k = slot_of(chip(-i if up else i))
        remote(rbuf.at[k], rbuf.at[k], fsend.at[k], erecv.at[k], partner).wait_recv()
        if i + STRIDE <= (up_reach if up else down_reach):
            onward(k, up).start()

    def step_of(source):
        up = lax.rem(z + nz - source, nz)
        away = jnp.where(up <= up_reach, up, nz - up)
        return jnp.where(up == 0, 0, (away - 1) // STRIDE)

    def source_of(g, i):
        return lax.rem(quad + quads - g, quads) * STRIDE + i

    def back(g, i):
        k = g * STRIDE + i
        to = {"dp": source_of(g, i) * 2 + core}
        return remote(sbuf.at[k], res.at[z], rsend.at[k], rrecv.at[z], to)

    sub = lax.broadcasted_iota(jnp.int32, (STRIDE, 8, 128), 1) < 4

    def score(g):
        held = rbuf[pl.ds(g * STRIDE, STRIDE)].reshape(STRIDE * own_rows, 4 * rank)
        prods = []
        for i in range(STRIDE):
            w = qbuf[:, :, i * 256 : (i + 1) * 256].reshape(-1, 256)
            pr = lax.dot_general(held, w, NT, preferred_element_type=F32)
            pr = pr.reshape(STRIDE, own_rows, pr.shape[-1])
            prods.append(pr[:, 8 * (i // 2) : 8 * (i // 2) + 8])
        packed = []
        for h in range(2):
            c0, c1 = h * 128, (h + 1) * 128
            s = jnp.where(sub, prods[0][:, :, c0:c1], prods[1][:, :, c0:c1])
            s = s + jnp.where(sub, prods[2][:, :, c0:c1], prods[3][:, :, c0:c1])
            packed.append(s + pltpu.roll(s, 4, 1))
        sbuf[pl.ds(g * STRIDE, STRIDE)] = jnp.where(sub, packed[0], packed[1]).astype(BF16)

        def send(i, carry):
            pl.when(source_of(g, i) != z)(lambda: back(g, i).start())
            return carry

        lax.fori_loop(0, STRIDE, send, 0)

    def score_step(step):
        def visit(g, carry):
            done = jnp.maximum(step_of(source_of(g, 0)), step_of(source_of(g, STRIDE - 1)))
            pl.when(done == step)(lambda: score(g))
            return carry

        lax.fori_loop(0, quads, visit, 0)

    passed = []
    for step in range(r_groups):
        for t in range(1, STRIDE + 1):
            if step == 0:
                pl.when(z == t - 1)(after_wrap)
            take(step * STRIDE + t, True)
        if step == 0:
            for k, dz in enumerate((-1, 1, 2)):
                came = lax.rem(z + nz + dz, STRIDE) * 2 + core
                q_sends[k].wait_recv()
                passed.append(
                    remote(
                        qbuf.at[came], qbuf.at[came], qsend.at[4 + k], qrecv.at[4 + k], partner
                    )
                )
                passed[-1].start()
        for t in range(1, STRIDE + 1):
            if step * STRIDE + t <= down_reach:
                take(step * STRIDE + t, False)
        if step == 0:
            q_near.wait_recv()
            for cp in passed:
                cp.wait_recv()
        score_step(step)
    res[z] = sbuf[part]

    for cp in q_sends + passed + ups + downs:
        cp.wait_send()

    def settle(i, carry):
        source = chip(-i)
        k = slot_of(source)
        pl.when(i + STRIDE <= up_reach)(lambda: onward(k, True).wait_send())
        pl.when((nz - i) + STRIDE <= down_reach)(lambda: onward(k, False).wait_send())
        back(k // STRIDE, lax.rem(k, STRIDE)).wait_send()
        return carry

    lax.fori_loop(1, nz, settle, 0)

    def collect(dz, carry):
        src = chip(dz)
        remote(res.at[src], res.at[src], rsend.at[0], rrecv.at[src], partner).wait_recv()
        return carry

    lax.fori_loop(1, nz, collect, 0)

    row = lax.broadcasted_iota(jnp.int32, (8, 128), 0)
    lane = lax.broadcasted_iota(jnp.int32, (8, 128), 1)
    col = (row // 4) * 128 + lane
    masks = []
    for rho in range(STRIDE):
        gap = (col // 64 - rho + STRIDE) & (STRIDE - 1)
        shift = jnp.where(gap == 3, -1, gap)
        shift = jnp.where(gap == 2, jnp.where((col // 32) % 2 == 0, -2, 2), shift)
        target = rho + shift
        masks.append((rho, 0, (target >= 0) & (target < STRIDE)))
        if rho < 2:
            masks.append((rho, -1, target < 0))
        else:
            masks.append((rho, 1, target >= STRIDE))

    def add_up(seg, carry):
        total = jnp.zeros((8, 128), F32)
        for rho, rel, mask in masks:
            val = res[lax.rem(seg + quads - rel, quads) * STRIDE + rho].astype(F32)
            total = total + jnp.where(mask, val, 0.0)
        out[seg] = total.astype(out.dtype)
        return carry

    lax.fori_loop(0, quads, add_up, 0)


def local(nz, activations, out_grads, lengths, proj_in, proj_out, queries):
    toks, ff = activations.shape
    d = out_grads.shape[1]
    rank = proj_in.shape[1]
    nq, params = queries.shape
    chunk = min(2048, d)
    n_loc = 1 + len(cuts(d, chunk)) + 2 * len(cuts(ff, chunk))
    dma = pltpu.SemaphoreType.DMA
    anyspec = pl.BlockSpec(memory_space=pl.ANY)
    rows = rank // STRIDE
    scores = pl.pallas_call(
        functools.partial(kernel, nz, chunk),
        out_shape=jax.ShapeDtypeStruct((nz // STRIDE, 8, 128), BF16),
        in_specs=[
            anyspec, anyspec, pl.BlockSpec(memory_space=pltpu.SMEM), anyspec, anyspec, anyspec,
        ],
        out_specs=pl.BlockSpec(memory_space=pltpu.VMEM),
        scratch_shapes=[
            pltpu.VMEM((toks, ff), BF16),
            pltpu.VMEM((toks, d), BF16),
            pltpu.VMEM((rank, ff), BF16),
            pltpu.VMEM((rank, d), BF16),
            pltpu.VMEM((nq, params), BF16),
            pltpu.VMEM((2 * STRIDE, nq, params // STRIDE), BF16),
            pltpu.VMEM((STRIDE, rows, 4 * rank), BF16),
            pltpu.VMEM((nz, rows, 4 * rank), BF16),
            pltpu.VMEM((nz, 8, 128), BF16),
            pltpu.VMEM((nz, 8, 128), BF16),
            dma((n_loc,)), dma((2,)), dma((7,)), dma((7,)), dma((2 * STRIDE,)),
            dma((nz,)), dma((nz,)), dma((nz,)), dma((nz,)), pltpu.SemaphoreType.REGULAR,
            pltpu.VMEM((2, toks, 2 * rank), F32),
            pltpu.VMEM((2, toks, 2 * rank), F32),
        ],
        compiler_params=pltpu.CompilerParams(collective_id=0, has_side_effects=True),
        name="score",
    )(activations, out_grads, lengths, proj_in.T, proj_out.T, queries)
    scores = scores.reshape(nz // STRIDE, 2, 4, 128).transpose(2, 0, 1, 3)
    return scores.reshape(lengths.shape[1], 2 * nz * nq)


def solution(mesh):
    both = P(("parts", "dp"), None)
    in_specs = (both, both, both, P(), P(), both)
    body = functools.partial(local, mesh.shape["dp"] // 2)
    return jax.shard_map(body, mesh=mesh, in_specs=in_specs, out_specs=both, check_vma=False)
```

time: 69.7 us -> 67.6 us (0.970)
  the two profiles are of different devices: /device:TPU:44 before, /device:TPU:100 now
where the time goes in v4:
time: 67.6 us; the launch traced here: 67.5 us
  Pallas kernels  66.1 us (98%)
  local copies, waits for them, and re-layouts  1.33 us (2%)
    pallas_call x1, Pallas kernels, local(): pl.pallas_call(functools.partial(kernel, nz, chunk), out_shape=jax.ShapeD...  66.1 us

profile of v4, /device:TPU:100, one launch (start us, length us, event | category | flops | bytes accessed | tf_op | source)
XLA Modules:
  0.0 67.5 jit_solution(9279262375555877357)
XLA Ops:
  0.0 66.1 %score.1 = bf16[8,8,128]{2,1,0:T(8,128)(2,1)} custom-call(bf16[256,14336]{1,0:T(8,128)(2,1)} %acts.1, bf16[256,4096]{1,0:T(8,128)(2,1)} %grads.1, s32[1,4]{1,0:T(1,128)} %lens.1, bf16[64,14336]{1,0:T(8,128)(2,1)} %bitcast.7, bf16[64,4096]{1,0:T(8,128)(2,1)} %bitcast.8, bf16[32,4096]{1,0:T(8,128)(2,1)} %qs.1), custom_call_target="tpu_custom_call" | custom-call | tf_op jit(solution)/shard_map/score/pallas_call | solution.py:352
  66.1 1.3 %copy.9 = bf16[4,2048]{1,0:T(4,128)(2,1)} copy(bf16[4,2048]{1,0:T(4,128)(2,1)} %bitcast.9) | data formatting | bytes 32768

commit v5 on v4

--- a/solution.py
+++ b/solution.py
@@ -24,20 +24,14 @@
     return list(zip(starts, widths))
 
 
-def split(nz):
-    total = nz // STRIDE
-    return total - total // 2, total // 2
-
-
 def kernel(
     nz, chunk, acts, grads, lens, pin, pout, qs, out,
-    abuf, gbuf, pinb, poutb, qv, qbuf, ybuf, rbuf, sbuf, res,
+    abuf, gbuf, pinb, poutb, qbuf, ybuf, rbuf, sbuf, res,
     loc_sem, qloc_sem, qsend, qrecv, dsend, fsend, erecv, rsend, rrecv, wrap_sem, pg_sum, pa_sum,
 ):
     me = lax.axis_index("dp")
     z, core = me // 2, lax.rem(me, 2)
     part = lax.rem(z, STRIDE)
-    r_groups, l_groups = split(nz)
     toks, ff = acts.shape
     d = grads.shape[1]
     rank = pin.shape[0]
@@ -72,21 +66,28 @@
         cp.start()
         n_sem += 1
         g_chunks.append((lo, w, cp))
-    q_all = pltpu.make_async_copy(qs, qv, qloc_sem.at[0])
-    q_own = pltpu.make_async_copy(qs.at[:, q_cols(0)], qbuf.at[part * 2 + core], qloc_sem.at[1])
-    q_all.start()
+    q_own = pltpu.make_async_copy(qs.at[:, q_cols(0)], qbuf.at[part * 2 + core], qloc_sem)
     q_own.start()
-    for lo, w in cuts(ff, chunk):
-        cp0 = pltpu.make_async_copy(
-            pin.at[:, pl.ds(lo, w)], pinb.at[:, pl.ds(lo, w)], loc_sem.at[n_sem]
+    pieces = cuts(ff, chunk)
+    middle = pieces[len(pieces) // 2][0]
+    halves = {0: slice(0, middle), middle: slice(middle, ff)}
+    for lo, w in pieces:
+        waits = []
+        if lo in halves:
+            cols = halves[lo]
+            waits.append(
+                pltpu.make_async_copy(pin.at[:, cols], pinb.at[:, cols], loc_sem.at[n_sem])
+            )
+            n_sem += 1
+        waits.append(
+            pltpu.make_async_copy(
+                acts.at[:, pl.ds(lo, w)], abuf.at[:, pl.ds(lo, w)], loc_sem.at[n_sem]
+            )
         )
-        cp1 = pltpu.make_async_copy(
-            acts.at[:, pl.ds(lo, w)], abuf.at[:, pl.ds(lo, w)], loc_sem.at[n_sem + 1]
-        )
-        cp0.start()
-        cp1.start()
-        n_sem += 2
-        a_chunks.append((lo, w, cp0, cp1))
+        n_sem += 1
+        for cp in waits:
+            cp.start()
+        a_chunks.append((lo, w, waits))
 
     barrier = pltpu.get_barrier_semaphore()
     near = [dz for t in range(1, STRIDE + 1) for dz in (t, -t)]
@@ -144,22 +145,21 @@
     lhs = jnp.where(member, wide.reshape(rows // 8, 8, toks), 0.0).reshape(rows, toks).astype(BF16)
 
     slot = part * 2 + core
-    q_up = remote(qv.at[:, q_cols(1)], qbuf.at[slot], qsend.at[0], qrecv.at[0], dev(1))
-    q_down = remote(qv.at[:, q_cols(-1)], qbuf.at[slot], qsend.at[1], qrecv.at[1], dev(-1))
+    q_up = remote(qs.at[:, q_cols(1)], qbuf.at[slot], qsend, qrecv.at[0], dev(1))
+    q_down = remote(qs.at[:, q_cols(-1)], qbuf.at[slot], qsend, qrecv.at[1], dev(-1))
     far = {"dp": lax.rem(z + nz + 2 - 4 * core, nz) * 2 + core}
-    q_far = remote(qv.at[:, q_cols(2)], qbuf.at[slot], qsend.at[2], qrecv.at[2], far)
-    q_near = remote(qv.at[:, q_cols(0)], qbuf.at[slot], qsend.at[3], qrecv.at[3], partner)
+    q_far = remote(qs.at[:, q_cols(2)], qbuf.at[slot], qsend, qrecv.at[2], far)
+    q_near = remote(qs.at[:, q_cols(0)], qbuf.at[slot], qsend, qrecv.at[3], partner)
     q_sends = [q_up, q_down, q_far, q_near]
-    for n, (lo, w, cp0, cp1) in enumerate(a_chunks):
-        if n == min(2, len(a_chunks) - 1):
-            q_all.wait()
+    for n, (lo, w, waits) in enumerate(a_chunks):
+        if n == min(1, len(a_chunks) - 1):
             await_near()
             q_up.start()
             q_near.start()
             pl.when((z >= STRIDE) | (core == 0))(q_far.start)
             pl.when(z >= STRIDE)(q_down.start)
-        cp0.wait()
-        cp1.wait()
+        for cp in waits:
+            cp.wait()
         add_product(abuf, pinb, lo, w, pa_sum, 2)
     pa = pa_sum[0] + pa_sum[1]
     left = lax.broadcasted_iota(jnp.int32, (toks, 2 * rank), 1) < rank
@@ -174,23 +174,22 @@
     for s in range(STRIDE):
         ybuf[s] = y[s * own_rows : (s + 1) * own_rows]
 
-    quads = nz // STRIDE
-    quad = z // STRIDE
-
-    def slot_of(source):
-        return lax.rem(quad + quads - source // STRIDE, quads) * STRIDE + lax.rem(source, STRIDE)
+    groups, blocks = nz // (2 * STRIDE), 2 * STRIDE
+    own = nz - 1
+
+    def slot_of(i, up):
+        return (i - 1) // STRIDE * blocks + (0 if up else STRIDE) + (i - 1) % STRIDE
 
     def leg(up, t):
         dz = t if up else -t
-        k = lax.rem(chip(dz) // STRIDE + quads - quad, quads) * STRIDE + part
-        i = (0 if up else STRIDE) + t - 1
+        k = slot_of(t, up)
         return remote(
-            ybuf.at[lax.rem(z + nz + dz, STRIDE)], rbuf.at[k], dsend.at[i], erecv.at[k], dev(dz)
+            ybuf.at[lax.rem(z + nz + dz, STRIDE)], rbuf.at[k], dsend, erecv.at[k], dev(dz)
         )
 
     hops = range(STRIDE, 0, -1)
     ups = [leg(True, t) for t in hops]
-    downs = [leg(False, t) for t in hops if l_groups > 1 or t < STRIDE]
+    downs = [leg(False, t) for t in hops if slot_of(t, False) != own]
     for cp in ups:
         cp.start()
 
@@ -200,50 +199,37 @@
 
     def after_wrap():
         pl.semaphore_wait(wrap_sem, STRIDE - z)
+        start_downs()
         q_down.start()
         pl.when(core == 1)(q_far.start)
-        start_downs()
 
     pl.when(z >= STRIDE)(start_downs)
-    rbuf[part] = ybuf[part]
+    rbuf[own] = ybuf[part]
     q_own.wait()
 
-    up_reach, down_reach = r_groups * STRIDE, l_groups * STRIDE - 1
-
-    def onward(k, up):
-        nxt = lax.rem(k + (STRIDE if up else nz - STRIDE), nz)
-        return remote(
-            rbuf.at[k], rbuf.at[nxt], fsend.at[k], erecv.at[nxt], dev(STRIDE if up else -STRIDE)
-        )
-
     def take(i, up):
-        k = slot_of(chip(-i if up else i))
-        remote(rbuf.at[k], rbuf.at[k], fsend.at[k], erecv.at[k], partner).wait_recv()
-        if i + STRIDE <= (up_reach if up else down_reach):
-            onward(k, up).start()
-
-    def step_of(source):
-        up = lax.rem(z + nz - source, nz)
-        away = jnp.where(up <= up_reach, up, nz - up)
-        return jnp.where(up == 0, 0, (away - 1) // STRIDE)
-
-    def source_of(g, i):
-        return lax.rem(quad + quads - g, quads) * STRIDE + i
-
-    def back(g, i):
-        k = g * STRIDE + i
-        to = {"dp": source_of(g, i) * 2 + core}
-        return remote(sbuf.at[k], res.at[z], rsend.at[k], rrecv.at[z], to)
-
-    sub = lax.broadcasted_iota(jnp.int32, (STRIDE, 8, 128), 1) < 4
-
-    def score(g):
-        held = rbuf[pl.ds(g * STRIDE, STRIDE)].reshape(STRIDE * own_rows, 4 * rank)
+        k = slot_of(i, up)
+        remote(rbuf.at[k], rbuf.at[k], fsend, erecv.at[k], partner).wait_recv()
+        nxt = k + blocks
+        if nxt < own:
+            remote(
+                rbuf.at[k], rbuf.at[nxt], fsend, erecv.at[nxt],
+                dev(STRIDE if up else -STRIDE),
+            ).start()
+
+    sub = lax.broadcasted_iota(jnp.int32, (blocks, 8, 128), 1) < 4
+
+    def back(k, dz):
+        return remote(sbuf.at[k], res.at[z], rsend, rrecv, dev(dz))
+
+    def score(step):
+        slots = slice(step * blocks, (step + 1) * blocks)
+        held = rbuf[slots].reshape(blocks * own_rows, 4 * rank)
         prods = []
         for i in range(STRIDE):
             w = qbuf[:, :, i * 256 : (i + 1) * 256].reshape(-1, 256)
             pr = lax.dot_general(held, w, NT, preferred_element_type=F32)
-            pr = pr.reshape(STRIDE, own_rows, pr.shape[-1])
+            pr = pr.reshape(blocks, own_rows, pr.shape[-1])
             prods.append(pr[:, 8 * (i // 2) : 8 * (i // 2) + 8])
         packed = []
         for h in range(2):
@@ -251,24 +237,15 @@
             s = jnp.where(sub, prods[0][:, :, c0:c1], prods[1][:, :, c0:c1])
             s = s + jnp.where(sub, prods[2][:, :, c0:c1], prods[3][:, :, c0:c1])
             packed.append(s + pltpu.roll(s, 4, 1))
-        sbuf[pl.ds(g * STRIDE, STRIDE)] = jnp.where(sub, packed[0], packed[1]).astype(BF16)
-
-        def send(i, carry):
-            pl.when(source_of(g, i) != z)(lambda: back(g, i).start())
-            return carry
-
-        lax.fori_loop(0, STRIDE, send, 0)
-
-    def score_step(step):
-        def visit(g, carry):
-            done = jnp.maximum(step_of(source_of(g, 0)), step_of(source_of(g, STRIDE - 1)))
-            pl.when(done == step)(lambda: score(g))
-            return carry
-
-        lax.fori_loop(0, quads, visit, 0)
+        sbuf[slots] = jnp.where(sub, packed[0], packed[1]).astype(BF16)
+        for t in range(STRIDE, 0, -1):
+            i = step * STRIDE + t
+            back(slot_of(i, True), -i).start()
+            if slot_of(i, False) != own:
+                back(slot_of(i, False), i).start()
 
     passed = []
-    for step in range(r_groups):
+    for step in range(groups):
         for t in range(1, STRIDE + 1):
             if step == 0:
                 pl.when(z == t - 1)(after_wrap)
@@ -279,40 +256,33 @@
                 q_sends[k].wait_recv()
                 passed.append(
                     remote(
-                        qbuf.at[came], qbuf.at[came], qsend.at[4 + k], qrecv.at[4 + k], partner
+                        qbuf.at[came], qbuf.at[came], qsend, qrecv.at[4 + k], partner
                     )
                 )
                 passed[-1].start()
         for t in range(1, STRIDE + 1):
-            if step * STRIDE + t <= down_reach:
+            if slot_of(step * STRIDE + t, False) != own:
                 take(step * STRIDE + t, False)
         if step == 0:
             q_near.wait_recv()
             for cp in passed:
                 cp.wait_recv()
-        score_step(step)
-    res[z] = sbuf[part]
-
-    for cp in q_sends + passed + ups + downs:
-        cp.wait_send()
-
-    def settle(i, carry):
-        source = chip(-i)
-        k = slot_of(source)
-        pl.when(i + STRIDE <= up_reach)(lambda: onward(k, True).wait_send())
-        pl.when((nz - i) + STRIDE <= down_reach)(lambda: onward(k, False).wait_send())
-        back(k // STRIDE, lax.rem(k, STRIDE)).wait_send()
-        return carry
-
-    lax.fori_loop(1, nz, settle, 0)
-
-    def collect(dz, carry):
-        src = chip(dz)
-        remote(res.at[src], res.at[src], rsend.at[0], rrecv.at[src], partner).wait_recv()
-        return carry
-
-    lax.fori_loop(1, nz, collect, 0)
-
+        score(step)
+    res[z] = sbuf[own]
+
+    def sent(ref, count, sem):
+        many = ref.at[pl.ds(0, count)]
+        remote(many, many, sem, rrecv, partner).wait_send()
+
+    sent(qbuf, len(q_sends) + len(passed), qsend)
+    sent(rbuf, len(ups) + len(downs), dsend)
+    if own > blocks:
+        sent(rbuf, own - blocks, fsend)
+    sent(sbuf, own, rsend)
+    others = res.at[pl.ds(0, own)]
+    remote(others, others, rsend, rrecv, partner).wait_recv()
+
+    quads = nz // STRIDE
     row = lax.broadcasted_iota(jnp.int32, (8, 128), 0)
     lane = lax.broadcasted_iota(jnp.int32, (8, 128), 1)
     col = (row // 4) * 128 + lane
@@ -345,7 +315,7 @@
     rank = proj_in.shape[1]
     nq, params = queries.shape
     chunk = min(2048, d)
-    n_loc = 1 + len(cuts(d, chunk)) + 2 * len(cuts(ff, chunk))
+    n_loc = 3 + len(cuts(d, chunk)) + len(cuts(ff, chunk))
     dma = pltpu.SemaphoreType.DMA
     anyspec = pl.BlockSpec(memory_space=pl.ANY)
     rows = rank // STRIDE
@@ -361,14 +331,13 @@
             pltpu.VMEM((toks, d), BF16),
             pltpu.VMEM((rank, ff), BF16),
             pltpu.VMEM((rank, d), BF16),
-            pltpu.VMEM((nq, params), BF16),
             pltpu.VMEM((2 * STRIDE, nq, params // STRIDE), BF16),
             pltpu.VMEM((STRIDE, rows, 4 * rank), BF16),
             pltpu.VMEM((nz, rows, 4 * rank), BF16),
             pltpu.VMEM((nz, 8, 128), BF16),
             pltpu.VMEM((nz, 8, 128), BF16),
-            dma((n_loc,)), dma((2,)), dma((7,)), dma((7,)), dma((2 * STRIDE,)),
-            dma((nz,)), dma((nz,)), dma((nz,)), dma((nz,)), pltpu.SemaphoreType.REGULAR,
+            dma((n_loc,)), dma(()), dma(()), dma((7,)), dma(()),
+            dma(()), dma((nz,)), dma(()), dma(()), pltpu.SemaphoreType.REGULAR,
             pltpu.VMEM((2, toks, 2 * rank), F32),
             pltpu.VMEM((2, toks, 2 * rank), F32),
         ],

time: 67.6 us -> 64.4 us (0.953)
  the two profiles are of different devices: /device:TPU:100 before, /device:TPU:44 now
where the time goes in v5:
time: 64.4 us; the launch traced here: 64.2 us
  Pallas kernels  62.9 us (98%)
  local copies, waits for them, and re-layouts  1.33 us (2%)
    pallas_call x1, Pallas kernels, local(): pl.pallas_call(functools.partial(kernel, nz, chunk), out_shape=jax.ShapeD...  62.9 us
    unnamed x1, local copies, waits for them, and re-layouts  1.33 us

profile of v5, /device:TPU:44, one launch (start us, length us, event | category | flops | bytes accessed | tf_op | source)
XLA Modules:
  0.0 64.2 jit_solution(12674522315039282973)
XLA Ops:
  0.0 62.9 %score.1 = bf16[8,8,128]{2,1,0:T(8,128)(2,1)} custom-call(bf16[256,14336]{1,0:T(8,128)(2,1)} %acts.1, bf16[256,4096]{1,0:T(8,128)(2,1)} %grads.1, s32[1,4]{1,0:T(1,128)} %lens.1, bf16[64,14336]{1,0:T(8,128)(2,1)} %bitcast.7, bf16[64,4096]{1,0:T(8,128)(2,1)} %bitcast.8, bf16[32,4096]{1,0:T(8,128)(2,1)} %qs.1), custom_call_target="tpu_custom_call" | custom-call | tf_op jit(solution)/shard_map/score/pallas_call | solution.py:322
  62.9 1.3 %copy.9 = bf16[4,2048]{1,0:T(4,128)(2,1)} copy(bf16[4,2048]{1,0:T(4,128)(2,1)} %bitcast.9) | data formatting | bytes 32768

commit v6 on v5

--- a/solution.py
+++ b/solution.py
@@ -40,8 +40,10 @@
     def chip(dz):
         return lax.rem(z + nz + dz, nz)
 
-    def dev(dz):
-        return {"dp": chip(dz) * 2 + core}
+    def dev(dz, c=1):
+        return {"dp": chip(dz) * 2 + c}
+
+    relays = core == 1
 
     partner = {"dp": z * 2 + 1 - core}
 
@@ -67,7 +69,7 @@
         n_sem += 1
         g_chunks.append((lo, w, cp))
     q_own = pltpu.make_async_copy(qs.at[:, q_cols(0)], qbuf.at[part * 2 + core], qloc_sem)
-    q_own.start()
+    pl.when(core == 1)(q_own.start)
     pieces = cuts(ff, chunk)
     middle = pieces[len(pieces) // 2][0]
     halves = {0: slice(0, middle), middle: slice(middle, ff)}
@@ -92,20 +94,18 @@
     barrier = pltpu.get_barrier_semaphore()
     near = [dz for t in range(1, STRIDE + 1) for dz in (t, -t)]
 
-    def greet(sem, dz):
-        pl.semaphore_signal(sem, inc=1, device_id=dev(dz), device_id_type=MESH)
+    def greet(sem, dz, cores):
+        for c in cores:
+            pl.semaphore_signal(sem, inc=1, device_id=dev(dz, c), device_id_type=MESH)
 
     for dz in near:
-        if dz < 0:
-            greet(barrier, dz)
-        else:
-            pl.when(z + dz < nz)(functools.partial(greet, barrier, dz))
+        pl.when(relays & (z + dz < nz))(functools.partial(greet, barrier, dz, (0, 1)))
     pl.semaphore_signal(barrier, inc=1, device_id=partner, device_id_type=MESH)
 
     def await_near():
         pl.semaphore_wait(barrier, len(near) + 1 - jnp.maximum(STRIDE - z, 0))
         for dz in range(1, STRIDE + 1):
-            pl.when(z + dz >= nz)(functools.partial(greet, wrap_sem, dz))
+            pl.when(relays & (z + dz >= nz))(functools.partial(greet, wrap_sem, dz, (1,)))
 
     def add_product(x_ref, w_ref, lo, w, total, copies):
         for i in range(2):
@@ -145,17 +145,18 @@
     lhs = jnp.where(member, wide.reshape(rows // 8, 8, toks), 0.0).reshape(rows, toks).astype(BF16)
 
     slot = part * 2 + core
-    q_up = remote(qs.at[:, q_cols(1)], qbuf.at[slot], qsend, qrecv.at[0], dev(1))
-    q_down = remote(qs.at[:, q_cols(-1)], qbuf.at[slot], qsend, qrecv.at[1], dev(-1))
-    far = {"dp": lax.rem(z + nz + 2 - 4 * core, nz) * 2 + core}
-    q_far = remote(qs.at[:, q_cols(2)], qbuf.at[slot], qsend, qrecv.at[2], far)
-    q_near = remote(qs.at[:, q_cols(0)], qbuf.at[slot], qsend, qrecv.at[3], partner)
-    q_sends = [q_up, q_down, q_far, q_near]
+    def q_send(dz, index, to):
+        return remote(qs.at[:, q_cols(dz)], qbuf.at[slot], qsend, qrecv.at[index], to)
+
+    q_up = q_send(1, core, dev(1))
+    q_down = q_send(-1, 2 + core, dev(-1))
+    q_far = q_send(2, 4 + core, {"dp": lax.rem(z + nz + 2 - 4 * core, nz) * 2 + 1})
+    q_near = q_send(0, 6, partner)
     for n, (lo, w, waits) in enumerate(a_chunks):
         if n == min(1, len(a_chunks) - 1):
             await_near()
             q_up.start()
-            q_near.start()
+            pl.when(core == 0)(q_near.start)
             pl.when((z >= STRIDE) | (core == 0))(q_far.start)
             pl.when(z >= STRIDE)(q_down.start)
         for cp in waits:
@@ -182,7 +183,7 @@
 
     def leg(up, t):
         dz = t if up else -t
-        k = slot_of(t, up)
+        k = 2 * slot_of(t, up) + core
         return remote(
             ybuf.at[lax.rem(z + nz + dz, STRIDE)], rbuf.at[k], dsend, erecv.at[k], dev(dz)
         )
@@ -198,38 +199,44 @@
             cp.start()
 
     def after_wrap():
-        pl.semaphore_wait(wrap_sem, STRIDE - z)
+        pl.semaphore_wait(wrap_sem, core * (STRIDE - z) + (1 - core))
+
+        @pl.when(relays)
+        def _():
+            pl.semaphore_signal(wrap_sem, inc=1, device_id=partner, device_id_type=MESH)
+
         start_downs()
         q_down.start()
         pl.when(core == 1)(q_far.start)
 
     pl.when(z >= STRIDE)(start_downs)
-    rbuf[own] = ybuf[part]
-    q_own.wait()
+    aside = remote(ybuf.at[part], rbuf.at[2 * own], dsend, erecv.at[2 * own], partner)
 
     def take(i, up):
         k = slot_of(i, up)
-        remote(rbuf.at[k], rbuf.at[k], fsend, erecv.at[k], partner).wait_recv()
         nxt = k + blocks
-        if nxt < own:
-            remote(
-                rbuf.at[k], rbuf.at[nxt], fsend, erecv.at[nxt],
-                dev(STRIDE if up else -STRIDE),
-            ).start()
-
-    sub = lax.broadcasted_iota(jnp.int32, (blocks, 8, 128), 1) < 4
-
-    def back(k, dz):
-        return remote(sbuf.at[k], res.at[z], rsend, rrecv, dev(dz))
+        for c in (1, 0):
+            here = rbuf.at[2 * k + c]
+            remote(here, here, fsend, erecv.at[2 * k + c], partner).wait_recv()
+            if nxt < own:
+                there = 2 * nxt + c
+                remote(
+                    here, rbuf.at[there], fsend, erecv.at[there], dev(STRIDE if up else -STRIDE)
+                ).start()
+
+    def back(k, dz, c):
+        return remote(sbuf.at[2 * k + c], res.at[z], rsend, rrecv, dev(dz, c))
 
     def score(step):
-        slots = slice(step * blocks, (step + 1) * blocks)
-        held = rbuf[slots].reshape(blocks * own_rows, 4 * rank)
+        count = 2 * blocks
+        sub = lax.broadcasted_iota(jnp.int32, (count, 8, 128), 1) < 4
+        slots = slice(step * count, (step + 1) * count)
+        held = rbuf[slots].reshape(count * own_rows, 4 * rank)
         prods = []
         for i in range(STRIDE):
             w = qbuf[:, :, i * 256 : (i + 1) * 256].reshape(-1, 256)
             pr = lax.dot_general(held, w, NT, preferred_element_type=F32)
-            pr = pr.reshape(blocks, own_rows, pr.shape[-1])
+            pr = pr.reshape(count, own_rows, pr.shape[-1])
             prods.append(pr[:, 8 * (i // 2) : 8 * (i // 2) + 8])
         packed = []
         for h in range(2):
@@ -240,47 +247,54 @@
         sbuf[slots] = jnp.where(sub, packed[0], packed[1]).astype(BF16)
         for t in range(STRIDE, 0, -1):
             i = step * STRIDE + t
-            back(slot_of(i, True), -i).start()
-            if slot_of(i, False) != own:
-                back(slot_of(i, False), i).start()
-
-    passed = []
-    for step in range(groups):
-        for t in range(1, STRIDE + 1):
-            if step == 0:
-                pl.when(z == t - 1)(after_wrap)
-            take(step * STRIDE + t, True)
-        if step == 0:
-            for k, dz in enumerate((-1, 1, 2)):
-                came = lax.rem(z + nz + dz, STRIDE) * 2 + core
-                q_sends[k].wait_recv()
-                passed.append(
-                    remote(
-                        qbuf.at[came], qbuf.at[came], qsend, qrecv.at[4 + k], partner
-                    )
-                )
-                passed[-1].start()
-        for t in range(1, STRIDE + 1):
-            if slot_of(step * STRIDE + t, False) != own:
-                take(step * STRIDE + t, False)
-        if step == 0:
-            q_near.wait_recv()
-            for cp in passed:
-                cp.wait_recv()
-        score(step)
-    res[z] = sbuf[own]
+            for c in range(2):
+                back(slot_of(i, True), -i, c).start()
+                if slot_of(i, False) != own:
+                    back(slot_of(i, False), i, c).start()
 
     def sent(ref, count, sem):
         many = ref.at[pl.ds(0, count)]
         remote(many, many, sem, rrecv, partner).wait_send()
 
-    sent(qbuf, len(q_sends) + len(passed), qsend)
-    sent(rbuf, len(ups) + len(downs), dsend)
-    if own > blocks:
-        sent(rbuf, own - blocks, fsend)
-    sent(sbuf, own, rsend)
-    others = res.at[pl.ds(0, own)]
-    remote(others, others, rsend, rrecv, partner).wait_recv()
+    def returned(count):
+        many = res.at[pl.ds(0, count)]
+        remote(many, many, rsend, rrecv, partner).wait_recv()
+
+    @pl.when(core == 0)
+    def _():
+        aside.start()
+        pl.when(z < STRIDE)(after_wrap)
+        sent(qbuf, 4, qsend)
+        sent(rbuf, len(ups) + len(downs) + 1, dsend)
+        returned(nz)
+
+    @pl.when(core == 1)
+    def _():
+        rbuf[2 * own + 1] = ybuf[part]
+        q_own.wait()
+        for step in range(groups):
+            for t in range(1, STRIDE + 1):
+                if step == 0:
+                    pl.when(z == t - 1)(after_wrap)
+                take(step * STRIDE + t, True)
+            for t in range(1, STRIDE + 1):
+                if slot_of(step * STRIDE + t, False) != own:
+                    take(step * STRIDE + t, False)
+            if step == 0:
+                for k in range(7):
+                    remote(qbuf.at[k], qbuf.at[k], qsend, qrecv.at[k], partner).wait_recv()
+            if step == groups - 1:
+                aside.wait_recv()
+            score(step)
+        other = remote(sbuf.at[2 * own], res.at[z], rsend, rrecv, partner)
+        other.start()
+        res[z] = sbuf[2 * own + 1]
+        sent(qbuf, 3, qsend)
+        sent(rbuf, len(ups) + len(downs), dsend)
+        if own > blocks:
+            sent(rbuf, 2 * (own - blocks), fsend)
+        sent(sbuf, 2 * own + 1, rsend)
+        returned(own)
 
     quads = nz // STRIDE
     row = lax.broadcasted_iota(jnp.int32, (8, 128), 0)
@@ -333,11 +347,11 @@
             pltpu.VMEM((rank, d), BF16),
             pltpu.VMEM((2 * STRIDE, nq, params // STRIDE), BF16),
             pltpu.VMEM((STRIDE, rows, 4 * rank), BF16),
-            pltpu.VMEM((nz, rows, 4 * rank), BF16),
-            pltpu.VMEM((nz, 8, 128), BF16),
+            pltpu.VMEM((2 * nz, rows, 4 * rank), BF16),
+            pltpu.VMEM((2 * nz, 8, 128), BF16),
             pltpu.VMEM((nz, 8, 128), BF16),
             dma((n_loc,)), dma(()), dma(()), dma((7,)), dma(()),
-            dma(()), dma((nz,)), dma(()), dma(()), pltpu.SemaphoreType.REGULAR,
+            dma(()), dma((2 * nz,)), dma(()), dma(()), pltpu.SemaphoreType.REGULAR,
             pltpu.VMEM((2, toks, 2 * rank), F32),
             pltpu.VMEM((2, toks, 2 * rank), F32),
         ],

time: 64.4 us -> 65.3 us (1.014); the launches traced: 64.2 us -> 64.3 us
  no operation moved by 1% of the time
where the time goes in v6:
time: 65.3 us; the launch traced here: 64.3 us
  Pallas kernels  62.9 us (96%)
  local copies, waits for them, and re-layouts  1.33 us (2%)
    pallas_call x1, Pallas kernels, local(): pl.pallas_call(functools.partial(kernel, nz, chunk), out_shape=jax.ShapeD...  62.9 us
    unnamed x1, local copies, waits for them, and re-layouts  1.33 us

profile of v6, /device:TPU:44, one launch (start us, length us, event | category | flops | bytes accessed | tf_op | source)
XLA Modules:
  0.0 64.3 jit_solution(16526128332296345846)
XLA Ops:
  0.0 62.9 %score.1 = bf16[8,8,128]{2,1,0:T(8,128)(2,1)} custom-call(bf16[256,14336]{1,0:T(8,128)(2,1)} %acts.1, bf16[256,4096]{1,0:T(8,128)(2,1)} %grads.1, s32[1,4]{1,0:T(1,128)} %lens.1, bf16[64,14336]{1,0:T(8,128)(2,1)} %bitcast.7, bf16[64,4096]{1,0:T(8,128)(2,1)} %bitcast.8, bf16[32,4096]{1,0:T(8,128)(2,1)} %qs.1), custom_call_target="tpu_custom_call" | custom-call | tf_op jit(solution)/shard_map/score/pallas_call | solution.py:336
  62.9 1.3 %copy.9 = bf16[4,2048]{1,0:T(4,128)(2,1)} copy(bf16[4,2048]{1,0:T(4,128)(2,1)} %bitcast.9) | data formatting | bytes 32768

commit v7 on v5

--- a/solution.py
+++ b/solution.py
@@ -246,10 +246,32 @@
 
     passed = []
     for step in range(groups):
-        for t in range(1, STRIDE + 1):
+        def take_ups(step=step):
+            for t in range(1, STRIDE + 1):
+                take(step * STRIDE + t, True)
+
+        def take_downs(step=step):
+            for t in range(1, STRIDE + 1):
+                if slot_of(step * STRIDE + t, False) != own:
+                    take(step * STRIDE + t, False)
+
+        down_first = (z < nz // 2) & (z < (step + 1) * STRIDE)
+
+        def down_then_up(step=step):
             if step == 0:
-                pl.when(z == t - 1)(after_wrap)
-            take(step * STRIDE + t, True)
+                after_wrap()
+            take_downs(step)
+            take_ups(step)
+
+        def up_then_down(step=step):
+            take_ups(step)
+            take_downs(step)
+
+        if step < 2:
+            pl.when(down_first)(down_then_up)
+            pl.when(jnp.logical_not(down_first))(up_then_down)
+        else:
+            up_then_down(step)
         if step == 0:
             for k, dz in enumerate((-1, 1, 2)):
                 came = lax.rem(z + nz + dz, STRIDE) * 2 + core
@@ -260,9 +282,6 @@
                     )
                 )
                 passed[-1].start()
-        for t in range(1, STRIDE + 1):
-            if slot_of(step * STRIDE + t, False) != own:
-                take(step * STRIDE + t, False)
         if step == 0:
             q_near.wait_recv()
             for cp in passed:

time: 64.4 us -> 64.3 us (level)
  no operation moved by 1% of the time
where the time goes in v7:
time: 64.3 us; the launch traced here: 64.1 us
  Pallas kernels  62.8 us (98%)
  local copies, waits for them, and re-layouts  1.33 us (2%)
    pallas_call x1, Pallas kernels, local(): pl.pallas_call(functools.partial(kernel, nz, chunk), out_shape=jax.ShapeD...  62.8 us
    unnamed x1, local copies, waits for them, and re-layouts  1.33 us

profile of v7, /device:TPU:44, one launch (start us, length us, event | category | flops | bytes accessed | tf_op | source)
XLA Modules:
  0.0 64.1 jit_solution(5819440946052444744)
XLA Ops:
  0.0 62.8 %score.1 = bf16[8,8,128]{2,1,0:T(8,128)(2,1)} custom-call(bf16[256,14336]{1,0:T(8,128)(2,1)} %acts.1, bf16[256,4096]{1,0:T(8,128)(2,1)} %grads.1, s32[1,4]{1,0:T(1,128)} %lens.1, bf16[64,14336]{1,0:T(8,128)(2,1)} %bitcast.7, bf16[64,4096]{1,0:T(8,128)(2,1)} %bitcast.8, bf16[32,4096]{1,0:T(8,128)(2,1)} %qs.1), custom_call_target="tpu_custom_call" | custom-call | tf_op jit(solution)/shard_map/score/pallas_call | solution.py:341
  62.8 1.3 %copy.9 = bf16[4,2048]{1,0:T(4,128)(2,1)} copy(bf16[4,2048]{1,0:T(4,128)(2,1)} %bitcast.9) | data formatting | bytes 32768
